TPU v7x, 32 devices: a whole 2x2x4 slice. The times are simulated.
32 devices in a mesh: section: 4 (over z), dp: 4 (over y, x), mp: 2 (over core).
Axes of the slice: x: 2, y: 2, z: 4, core: 2. Of those that a mesh axis runs over, the one named last changes fastest.
Arguments:
- fwd_in: bfloat16 [4, 2048, 1024], P('section', ('dp', 'mp')), may hold values from -6 to 6
- stash: bfloat16 [4, 2048, 1024], P('section', ('dp', 'mp')), may hold values from -6 to 6
- cot: bfloat16 [4, 2048, 1024], P('section', ('dp', 'mp')), may hold values from -8 to 8
- w_in: bfloat16 [4, 2048, 1024], P('section', 'mp'), may hold values from -0.1875 to 0.1875
- w_out: bfloat16 [4, 2048, 1024], P('section', 'mp'), may hold values from -0.125 to 0.125
- gain: float32 [4, 1024], P('section'), may hold values from 0.1 to 1.9
Outputs:
- passed_fwd: bfloat16 [4, 2048, 1024], P('section', ('dp', 'mp'))
- passed_grad: bfloat16 [4, 2048, 1024], P('section', ('dp', 'mp'))
- grad_w_in: bfloat16 [4, 2048, 1024], P('section', 'mp', 'dp')
- grad_w_out: bfloat16 [4, 2048, 1024], P('section', 'mp', 'dp')
All inputs are finite; a program needn't handle non-finite values.
Results may differ from a plain program's by a relative error of at most 0.015.
Values may be sent and summed in bfloat16 or wider, within the bound.
A program may use at most 64 MiB of HBM per device.

v0:
```python
import jax
import jax.numpy as jnp
from jax import lax
from jax.experimental import pallas as pl
from jax.experimental.pallas import tpu as pltpu
from jax.sharding import PartitionSpec as P

norm_eps = 1e-05
gelu_coef = 0.7978845608


def shifted(x, axis, by):
    length = lax.axis_size(axis)
    return lax.ppermute(x, axis, [(i, (i + by) % length) for i in range(length)])


def gelu_value(v):
    inner = jnp.tanh(gelu_coef * (v + 0.044715 * v * v * v))
    return 0.5 * v * (1.0 + inner)


def gelu_slope(v):
    inner = jnp.tanh(gelu_coef * (v + 0.044715 * v * v * v))
    return 0.5 * (1.0 + inner) + 0.5 * v * (1.0 - inner * inner) * gelu_coef * (
        1.0 + 0.134145 * v * v
    )


def prepare(x, w_first, gain_row):
    xf = x.astype(jnp.float32)
    scale = lax.rsqrt(jnp.mean(xf * xf, axis=-1, keepdims=True) + norm_eps)
    normed = (xf * scale * gain_row[None, :]).astype(jnp.bfloat16)
    pre = lax.dot_general(
        normed, w_first, (((1,), (1,)), ((), ())), preferred_element_type=jnp.float32
    )
    act = gelu_value(pre).astype(jnp.bfloat16)
    return (scale, normed, pre, act)


def on_device(fwd_in, stash, cot, w_in, w_out, gain):
    x_fwd = fwd_in[0]
    x_bwd = stash[0]
    cot_local = cot[0]
    w_first = w_in[0]
    w_second = w_out[0]
    gain_row = gain[0]
    local_rows = x_fwd.shape[0]
    scale, normed, pre, act = prepare(
        lax.all_gather(x_fwd, "mp", axis=0, tiled=True), w_first, gain_row
    )
    terms = jnp.dot(act, w_second, preferred_element_type=jnp.float32)
    branch = lax.psum_scatter(
        terms.astype(jnp.bfloat16), "mp", scatter_dimension=0, tiled=True
    ).astype(jnp.float32)
    out = (x_fwd.astype(jnp.float32) + branch).astype(jnp.bfloat16)
    passed_fwd = shifted(out, "section", 1)
    rows_x, rows_cot = (
        lax.all_gather(x_bwd, "mp", axis=0, tiled=True),
        lax.all_gather(cot_local, "mp", axis=0, tiled=True),
    )
    scale, normed, pre, act = prepare(rows_x, w_first, gain_row)
    d_act = lax.dot_general(
        rows_cot, w_second, (((1,), (1,)), ((), ())), preferred_element_type=jnp.float32
    )
    d_pre = (d_act * gelu_slope(pre)).astype(jnp.bfloat16)
    d_norm = lax.psum_scatter(
        jnp.dot(d_pre, w_first, preferred_element_type=jnp.float32).astype(jnp.bfloat16),
        "mp",
        scatter_dimension=0,
        tiled=True,
    ).astype(jnp.float32)
    offset = lax.axis_index("mp") * local_rows
    own_scale = lax.dynamic_slice_in_dim(scale, offset, local_rows, 0)
    shard_x = x_bwd.astype(jnp.float32)
    push = d_norm * gain_row[None, :]
    mixed = jnp.mean(shard_x * push, axis=-1, keepdims=True)
    dx = (
        cot_local.astype(jnp.float32)
        + own_scale * push
        - shard_x * own_scale * own_scale * own_scale * mixed
    )
    passed_grad = shifted(dx.astype(jnp.bfloat16), "section", -1)
    term_out = lax.dot_general(
        act, rows_cot, (((0,), (0,)), ((), ())), preferred_element_type=jnp.float32
    )
    term_in = lax.dot_general(
        d_pre, normed, (((0,), (0,)), ((), ())), preferred_element_type=jnp.float32
    )
    sum_in, sum_out = (
        lax.psum_scatter(
            term_in.astype(jnp.bfloat16), "dp", scatter_dimension=1, tiled=True
        ).astype(jnp.float32),
        lax.psum_scatter(
            term_out.astype(jnp.bfloat16), "dp", scatter_dimension=1, tiled=True
        ).astype(jnp.float32),
    )
    return (
        passed_fwd[None],
        passed_grad[None],
        sum_in.astype(jnp.bfloat16)[None],
        sum_out.astype(jnp.bfloat16)[None],
    )


MESH = pl.DeviceIdType.MESH
vmem_bytes = 67_043_328
NT = (((1,), (1,)), ((), ()))
TN = (((0,), (0,)), ((), ()))
DIAG, DIRECT, SECOND, OWN = range(4)
OUT, IN = range(2)


def tile_of(total, most):
    size = min(total, most)
    while total % size:
        size //= 2
    return size


def start_remote(src, dst, send, recv, target):
    copy = pltpu.make_async_remote_copy(
        src_ref=src, dst_ref=dst, send_sem=send, recv_sem=recv,
        device_id=target, device_id_type=MESH,
    )
    copy.start()
    return copy


def greet(targets):
    barrier = pltpu.get_barrier_semaphore()
    for target in targets:
        pl.semaphore_signal(barrier, inc=1, device_id=target, device_id_type=MESH)
    return barrier


def swap_kernel(
    fwd_hbm, stash_hbm, cot_hbm, win_hbm, wout_hbm,
    xs, xc, xf, win, wout,
    load_sem, send_sem, recv_sem,
):
    rows = stash_hbm.shape[0]
    peer = {"mp": 1 - lax.axis_index("mp")}
    barrier = greet([peer])
    own, other = pl.ds(0, rows), pl.ds(rows, rows)
    shared = ((stash_hbm, xs), (cot_hbm, xc))
    whole = ((win_hbm, win), (fwd_hbm, xf), (wout_hbm, wout))
    pairs = [*((src, dst.at[own]) for src, dst in shared), *whole]
    loads = [
        pltpu.make_async_copy(src, dst, load_sem.at[i]) for i, (src, dst) in enumerate(pairs)
    ]
    pl.semaphore_wait(barrier, 1)
    swaps = [
        start_remote(src, dst.at[other], send_sem.at[i], recv_sem.at[i], peer)
        for i, (src, dst) in enumerate(shared)
    ]
    for load in loads:
        load.start()
    for load in loads:
        load.wait()
    for swap in swaps:
        swap.wait()


def write_kernel(a, b, c, d, a_out, b_out, c_out, d_out, sems):
    copies = [
        pltpu.make_async_copy(src, dst, sems.at[i])
        for i, (src, dst) in enumerate(((a, a_out), (b, b_out), (c, c_out), (d, d_out)))
    ]
    for copy in copies:
        copy.start()
    for copy in copies:
        copy.wait()


def relay_kernel(
    xs, xc, xf, win, wout, gain_ref,
    pass_fwd, pass_grad, gin_ref, gout_ref,
    xf_peer, nb, nf, slope, act_t, dpre_t, act, parts, landed,
    mp_out, mp_in, own_terms, z_out,
    mp_send, mp_recv, rs_send, rs_recv, z_send, z_recv,
):
    rows = pass_fwd.shape[0]
    hid, width = win.shape
    half = hid // 2
    cols = gin_ref.shape[1]
    n_sec = lax.axis_size("section")
    sec, dp, mp = lax.axis_index("section"), lax.axis_index("dp"), lax.axis_index("mp")
    y, x = lax.div(dp, 2), lax.rem(dp, 2)
    flip_x, flip_y = y * 2 + (1 - x), (1 - y) * 2 + x
    across = (1 - y) * 2 + (1 - x)
    peer = {"mp": 1 - mp}
    after, before = {"section": lax.rem(sec + 1, n_sec)}, {"section": lax.rem(sec + n_sec - 1, n_sec)}
    barrier = greet([after, before, {"dp": flip_x}, {"dp": flip_y}, peer])

    own, other = pl.ds(0, rows), pl.ds(rows, rows)
    gain = gain_ref[...]
    step = tile_of(rows, 64)

    def normalise(source, target, first, skip=0):
        def body(i, carry):
            at = pl.ds(pl.multiple_of(first + i * step, step), step)
            v = source[pl.ds(pl.multiple_of(first - skip + i * step, step), step), :].astype(jnp.float32)
            r = lax.rsqrt(jnp.mean(v * v, axis=-1, keepdims=True) + norm_eps)
            target[at, :] = (v * r * gain).astype(jnp.bfloat16)
            return carry

        lax.fori_loop(0, rows // step, body, 0)

    block = tile_of(half, 256)

    def backward_pre(first, count):
        def body(i, carry):
            at = pl.ds(pl.multiple_of(first + i * block, block), block)
            v = lax.dot_general(
                win[at, :], nb[...], NT, preferred_element_type=jnp.float32
            )
            square = v * v
            t = jnp.tanh(gelu_coef * (v + 0.044715 * square * v))
            act_t[at, :] = (0.5 * v * (1.0 + t)).astype(jnp.bfloat16)
            slope[at, :] = 0.5 * (1.0 + t) + 0.5 * v * (1.0 - t * t) * gelu_coef * (
                1.0 + 0.134145 * square
            )
            return carry

        lax.fori_loop(0, count // block, body, 0)

    def backward_slope(first, count):
        def body(i, carry):
            at = pl.ds(pl.multiple_of(first + i * block, block), block)
            d_act = lax.dot_general(
                wout[at, :], xc[...], NT, preferred_element_type=jnp.float32
            )
            dpre_t[at, :] = (d_act * slope[at, :]).astype(jnp.bfloat16)
            return carry

        lax.fori_loop(0, count // block, body, 0)

    owners = (
        (across, flip_x, flip_y, dp),
        (across, flip_y, flip_x, dp),
    )
    nearest = (({"dp": flip_x}, {"dp": flip_y}), ({"dp": flip_y}, {"dp": flip_x}))
    halves = [pl.ds(0, half), pl.ds(half, half)]
    operands = {OUT: (act_t, xc), IN: (dpre_t, nb)}

    def product(g, h, kind):
        left, right = operands[g]
        at = pl.ds(pl.multiple_of(owners[h][kind] * cols, cols), cols)
        parts[g, h, kind] = jnp.dot(
            left[halves[h], :], right[:, at], preferred_element_type=jnp.float32
        ).astype(jnp.bfloat16)

    sent = {}

    def send(g, h, kind):
        sent[g, h, kind] = start_remote(
            parts.at[g, h, kind], landed.at[g, h, kind],
            rs_send.at[g, h, kind], rs_recv.at[g, h, kind],
            nearest[h][1 if kind == SECOND else 0],
        )

    normalise(xs, nb, 0)
    normalise(xs, nb, rows)
    backward_pre(0, half)
    product(OUT, 0, DIAG)
    backward_pre(half, half)
    product(OUT, 1, DIAG)
    pl.semaphore_wait(barrier, 5)
    send(OUT, 0, DIAG)
    send(OUT, 1, DIAG)
    swap_fwd = start_remote(xf, xf_peer, mp_send.at[2], mp_recv.at[2], peer)
    for h in range(2):
        product(OUT, h, DIRECT)
        send(OUT, h, DIRECT)

    for h in range(2):
        backward_slope(h * half, half)
        product(IN, h, DIAG)
        send(IN, h, DIAG)
    for h in range(2):
        product(IN, h, DIRECT)
        send(IN, h, DIRECT)

    def d_norm(slot):
        return lax.dot_general(
            dpre_t[:, slot], win[...], TN, preferred_element_type=jnp.float32
        ).astype(jnp.bfloat16)

    mp_out[0] = d_norm(other)
    swap_grad = start_remote(mp_out.at[0], mp_in.at[0], mp_send.at[0], mp_recv.at[0], peer)
    own_terms[0] = d_norm(own)


    def forward(slot):
        def body(i, carry):
            at = pl.ds(pl.multiple_of(i * block, block), block)
            v = lax.dot_general(
                nf[slot, :], win[at, :], NT, preferred_element_type=jnp.float32
            )
            t = jnp.tanh(gelu_coef * (v + 0.044715 * v * v * v))
            act[:, at] = (0.5 * v * (1.0 + t)).astype(jnp.bfloat16)
            return carry

        lax.fori_loop(0, hid // block, body, 0)
        return jnp.dot(
            act[...], wout[...], preferred_element_type=jnp.float32
        ).astype(jnp.bfloat16)

    swap_grad.wait_recv()

    def finish_grad(i, carry):
        at = pl.ds(pl.multiple_of(i * step, step), step)
        v = xs[at, :].astype(jnp.float32)
        r = lax.rsqrt(jnp.mean(v * v, axis=-1, keepdims=True) + norm_eps)
        push = (own_terms[0, at, :].astype(jnp.float32) + mp_in[0, at, :].astype(jnp.float32)) * gain
        mixed = jnp.mean(v * push, axis=-1, keepdims=True)
        dx = xc[at, :].astype(jnp.float32) + r * push - v * (r * r * r * mixed)
        z_out[0, at, :] = dx.astype(jnp.bfloat16)
        return carry

    lax.fori_loop(0, rows // step, finish_grad, 0)
    relay_grad = start_remote(z_out.at[0], pass_grad, z_send.at[0], z_recv.at[0], before)

    swap_fwd.wait_recv()
    normalise(xf_peer, nf, rows, rows)
    mp_out[1] = forward(other)
    swap_branch = start_remote(mp_out.at[1], mp_in.at[1], mp_send.at[1], mp_recv.at[1], peer)
    normalise(xf, nf, 0)
    own_terms[1] = forward(own)
    swap_branch.wait_recv()

    def finish_forward(i, carry):
        at = pl.ds(pl.multiple_of(i * step, step), step)
        branch = own_terms[1, at, :].astype(jnp.float32) + mp_in[1, at, :].astype(jnp.float32)
        z_out[1, at, :] = (xf[at, :].astype(jnp.float32) + branch).astype(jnp.bfloat16)
        return carry

    lax.fori_loop(0, rows // step, finish_forward, 0)
    relay_fwd = start_remote(z_out.at[1], pass_fwd, z_send.at[1], z_recv.at[1], after)

    for g in (OUT, IN):
        for h in range(2):
            product(g, h, SECOND)
        for h in range(2):
            sent[g, h, DIAG].wait_recv()
            parts[g, h, SECOND] = (
                parts[g, h, SECOND].astype(jnp.float32) + landed[g, h, DIAG].astype(jnp.float32)
            ).astype(jnp.bfloat16)
            send(g, h, SECOND)
        for h in range(2):
            product(g, h, OWN)
    for g, result in ((OUT, gout_ref), (IN, gin_ref)):
        for h in range(2):
            sent[g, h, DIRECT].wait_recv()
            sent[g, h, SECOND].wait_recv()
            result[halves[h], :] = (
                parts[g, h, OWN].astype(jnp.float32)
                + landed[g, h, DIRECT].astype(jnp.float32)
                + landed[g, h, SECOND].astype(jnp.float32)
            ).astype(jnp.bfloat16)

    relay_grad.wait_recv()
    relay_fwd.wait_recv()
    for copy in [swap_fwd, swap_grad, swap_branch, relay_grad, relay_fwd, *sent.values()]:
        copy.wait_send()


def relay_on_device(fwd_in, stash, cot, w_in, w_out, gain):
    rows, width = stash.shape[1:]
    hid = w_in.shape[1]
    tokens = rows * lax.axis_size("mp")
    cols = width // lax.axis_size("dp")
    half = hid // 2
    bf16 = jnp.bfloat16
    vmem = pl.BlockSpec(memory_space=pltpu.VMEM)
    hbm = pl.BlockSpec(memory_space=pl.ANY)
    dma = pltpu.SemaphoreType.DMA
    held = (tokens * 2 + rows + hid * 2) * width * jnp.dtype(bf16).itemsize
    loaded = pl.pallas_call(
        swap_kernel,
        out_shape=(pltpu.VMEM((tokens, width), bf16),) * 2
        + (pltpu.VMEM((rows, width), bf16),)
        + (pltpu.VMEM((hid, width), bf16),) * 2,
        in_specs=[hbm] * 5,
        out_specs=(vmem,) * 5,
        scratch_shapes=[dma((5,)), dma((2,)), dma((2,))],
        compiler_params=pltpu.CompilerParams(
            collective_id=0, has_side_effects=True,
            vmem_limit_bytes=vmem_bytes - held - 2**17,
        ),
    )(fwd_in[0], stash[0], cot[0], w_in[0], w_out[0])
    results = pl.pallas_call(
        relay_kernel,
        out_shape=(pltpu.VMEM((rows, width), bf16),) * 2 + (pltpu.VMEM((hid, cols), bf16),) * 2,
        in_specs=[vmem] * 6,
        out_specs=(vmem,) * 4,
        scratch_shapes=[
            pltpu.VMEM((rows, width), bf16),
            pltpu.VMEM((tokens, width), bf16),
            pltpu.VMEM((tokens, width), bf16),
            pltpu.VMEM((hid, tokens), jnp.float32),
            pltpu.VMEM((hid, tokens), bf16),
            pltpu.VMEM((hid, tokens), bf16),
            pltpu.VMEM((rows, hid), bf16),
            pltpu.VMEM((2, 2, 4, half, cols), bf16),
            pltpu.VMEM((2, 2, 3, half, cols), bf16),
            pltpu.VMEM((2, rows, width), bf16),
            pltpu.VMEM((2, rows, width), bf16),
            pltpu.VMEM((2, rows, width), bf16),
            pltpu.VMEM((2, rows, width), bf16),
            dma((3,)),
            dma((3,)),
            dma((2, 2, 3)),
            dma((2, 2, 3)),
            dma((2,)),
            dma((2,)),
        ],
        compiler_params=pltpu.CompilerParams(
            collective_id=1, has_side_effects=True, vmem_limit_bytes=40 * 2**20
        ),
    )(*loaded, gain)
    results = pl.pallas_call(
        write_kernel,
        out_shape=tuple(jax.ShapeDtypeStruct(r.shape, r.dtype) for r in results),
        in_specs=[vmem] * 4,
        out_specs=(hbm,) * 4,
        scratch_shapes=[dma((4,))],
        compiler_params=pltpu.CompilerParams(vmem_limit_bytes=4 * 2**20),
    )(*results)
    return tuple(r[None] for r in results)


def fits_relay(mesh):
    return mesh.shape["dp"] == 4 and mesh.shape["mp"] == 2 and mesh.shape["section"] > 1


def solution(mesh):
    in_specs = (
        P("section", ("dp", "mp"), None),
        P("section", ("dp", "mp"), None),
        P("section", ("dp", "mp"), None),
        P("section", "mp", None),
        P("section", "mp", None),
        P("section", None),
    )
    out_specs = (
        P("section", ("dp", "mp"), None),
        P("section", ("dp", "mp"), None),
        P("section", "mp", "dp"),
        P("section", "mp", "dp"),
    )
    return jax.shard_map(
        relay_on_device if fits_relay(mesh) else on_device,
        mesh=mesh,
        in_specs=in_specs,
        out_specs=out_specs,
        check_vma=False,
    )
```

profile of v0, /device:TPU:0, one launch (start us, length us, event | category | flops | bytes accessed | tf_op | source)
XLA Modules:
  0.0 48.0 jit_solution(14129396857896834422)
XLA Ops:
  0.6 0.0 copy-start
  0.6 3.3 %shard_map.93 = (bf16[512,1024]{1,0:T(8,128)(2,1)S(1)}, bf16[512,1024]{1,0:T(8,128)(2,1)S(1)}, bf16[256,1024]{1,0:T(8,128)(2,1)S(1)}, bf16[1024,1024]{1,0:T(8,128)(2,1)S(1)}, bf16[1024,1024]{1,0:T(8,128)(2,1)S(1)}) custom-call(bf16[256,1024]{1,0:T(8,128)(2,1)} %bitcast.11, bf16[256,1024]{1,0:T(8,128)(2,1)} %bitcast.12, bf16[256,1024]{1,0:T(8,128)(2,1)} %bitcast.13, ...), custom_call_target="tpu_custom_call" | custom-call | tf_op jit(solution)/shard_map/pallas_call | solution.py:379
  4.0 0.0 copy-done
  4.0 42.6 %shard_map.94 = (bf16[256,1024]{1,0:T(8,128)(2,1)S(1)}, bf16[256,1024]{1,0:T(8,128)(2,1)S(1)}, bf16[1024,256]{1,0:T(8,128)(2,1)S(1)}, bf16[1024,256]{1,0:T(8,128)(2,1)S(1)}) custom-call(bf16[512,1024]{1,0:T(8,128)(2,1)S(1)} %get-tuple-element.17.xs, bf16[512,1024]{1,0:T(8,128)(2,1)S(1)} %get-tuple-element.18.xc, bf16[256,1024]{1,0:T(8,128)(2,1)S(1)} %get-tuple-element.19.xf, ...), custom_call_target="tpu_custom_call" | custom-call | tf_op jit(solution)/shard_map/pallas_call | solution.py:392
  46.6 1.3 %shard_map.95 = (bf16[256,1024]{1,0:T(8,128)(2,1)}, bf16[256,1024]{1,0:T(8,128)(2,1)}, bf16[1024,256]{1,0:T(8,128)(2,1)}, bf16[1024,256]{1,0:T(8,128)(2,1)}) custom-call(bf16[256,1024]{1,0:T(8,128)(2,1)S(1)} %get-tuple-element.22.a, bf16[256,1024]{1,0:T(8,128)(2,1)S(1)} %get-tuple-element.23.b, bf16[1024,256]{1,0:T(8,128)(2,1)S(1)} %get-tuple-element.24.c, ...), custom_call_target="tpu_custom_call" | custom-call | tf_op jit(solution)/shard_map/pallas_call | solution.py:422
Async XLA Ops:
  0.6 3.3 %copy-start = (f32[1,1024]{1,0:T(1,128)S(1)}, f32[1,1024]{1,0:T(1,128)}, u32[]{:S(2)}) copy-start(f32[1,1024]{1,0:T(1,128)} %gain_ref.1) | copy-start | bytes 12292
where the time goes:
time: 48.1 us; the launch traced here: 48 us
  Pallas kernels  47.3 us (98%)
  between operations  0.66 us (1%)
    pallas_call x1, Pallas kernels, relay_on_device(): pl.pallas_call(relay_kernel, out_shape=(pltpu.VMEM((rows, width), bf16),)...  42.6 us
    pallas_call x1, Pallas kernels, relay_on_device(): pl.pallas_call(swap_kernel, out_shape=(pltpu.VMEM((tokens, width), bf16),...  3.31 us
    pallas_call x1, Pallas kernels, relay_on_device(): pl.pallas_call(write_kernel, out_shape=tuple((jax.ShapeDtypeStruct(r.shap...  1.35 us

commit v1 on v0

v1 whole, which is shorter than its diff:
```python
import jax
import jax.numpy as jnp
from jax import lax
from jax.experimental import pallas as pl
from jax.experimental.pallas import tpu as pltpu
from jax.sharding import PartitionSpec as P

norm_eps = 1e-05
gelu_coef = 0.7978845608


def shifted(x, axis, by):
    length = lax.axis_size(axis)
    return lax.ppermute(x, axis, [(i, (i + by) % length) for i in range(length)])


def gelu_value(v):
    inner = jnp.tanh(gelu_coef * (v + 0.044715 * v * v * v))
    return 0.5 * v * (1.0 + inner)


def gelu_slope(v):
    inner = jnp.tanh(gelu_coef * (v + 0.044715 * v * v * v))
    return 0.5 * (1.0 + inner) + 0.5 * v * (1.0 - inner * inner) * gelu_coef * (
        1.0 + 0.134145 * v * v
    )


def prepare(x, w_first, gain_row):
    xf = x.astype(jnp.float32)
    scale = lax.rsqrt(jnp.mean(xf * xf, axis=-1, keepdims=True) + norm_eps)
    normed = (xf * scale * gain_row[None, :]).astype(jnp.bfloat16)
    pre = lax.dot_general(
        normed, w_first, (((1,), (1,)), ((), ())), preferred_element_type=jnp.float32
    )
    act = gelu_value(pre).astype(jnp.bfloat16)
    return (scale, normed, pre, act)


def on_device(fwd_in, stash, cot, w_in, w_out, gain):
    x_fwd = fwd_in[0]
    x_bwd = stash[0]
    cot_local = cot[0]
    w_first = w_in[0]
    w_second = w_out[0]
    gain_row = gain[0]
    local_rows = x_fwd.shape[0]
    scale, normed, pre, act = prepare(
        lax.all_gather(x_fwd, "mp", axis=0, tiled=True), w_first, gain_row
    )
    terms = jnp.dot(act, w_second, preferred_element_type=jnp.float32)
    branch = lax.psum_scatter(
        terms.astype(jnp.bfloat16), "mp", scatter_dimension=0, tiled=True
    ).astype(jnp.float32)
    out = (x_fwd.astype(jnp.float32) + branch).astype(jnp.bfloat16)
    passed_fwd = shifted(out, "section", 1)
    rows_x, rows_cot = (
        lax.all_gather(x_bwd, "mp", axis=0, tiled=True),
        lax.all_gather(cot_local, "mp", axis=0, tiled=True),
    )
    scale, normed, pre, act = prepare(rows_x, w_first, gain_row)
    d_act = lax.dot_general(
        rows_cot, w_second, (((1,), (1,)), ((), ())), preferred_element_type=jnp.float32
    )
    d_pre = (d_act * gelu_slope(pre)).astype(jnp.bfloat16)
    d_norm = lax.psum_scatter(
        jnp.dot(d_pre, w_first, preferred_element_type=jnp.float32).astype(jnp.bfloat16),
        "mp",
        scatter_dimension=0,
        tiled=True,
    ).astype(jnp.float32)
    offset = lax.axis_index("mp") * local_rows
    own_scale = lax.dynamic_slice_in_dim(scale, offset, local_rows, 0)
    shard_x = x_bwd.astype(jnp.float32)
    push = d_norm * gain_row[None, :]
    mixed = jnp.mean(shard_x * push, axis=-1, keepdims=True)
    dx = (
        cot_local.astype(jnp.float32)
        + own_scale * push
        - shard_x * own_scale * own_scale * own_scale * mixed
    )
    passed_grad = shifted(dx.astype(jnp.bfloat16), "section", -1)
    term_out = lax.dot_general(
        act, rows_cot, (((0,), (0,)), ((), ())), preferred_element_type=jnp.float32
    )
    term_in = lax.dot_general(
        d_pre, normed, (((0,), (0,)), ((), ())), preferred_element_type=jnp.float32
    )
    sum_in, sum_out = (
        lax.psum_scatter(
            term_in.astype(jnp.bfloat16), "dp", scatter_dimension=1, tiled=True
        ).astype(jnp.float32),
        lax.psum_scatter(
            term_out.astype(jnp.bfloat16), "dp", scatter_dimension=1, tiled=True
        ).astype(jnp.float32),
    )
    return (
        passed_fwd[None],
        passed_grad[None],
        sum_in.astype(jnp.bfloat16)[None],
        sum_out.astype(jnp.bfloat16)[None],
    )


MESH = pl.DeviceIdType.MESH
vmem_bytes = 67_043_328
NT = (((1,), (1,)), ((), ()))
TN = (((0,), (0,)), ((), ()))
OUT, IN = range(2)
pieces = 2


def tile_of(total, most):
    size = min(total, most)
    while total % size:
        size //= 2
    return size


def remote(src, dst, send, recv, target):
    return pltpu.make_async_remote_copy(
        src_ref=src, dst_ref=dst, send_sem=send, recv_sem=recv,
        device_id=target, device_id_type=MESH,
    )


def start_remote(src, dst, send, recv, target):
    copy = remote(src, dst, send, recv, target)
    copy.start()
    return copy


def write_kernel(a, b, c, d, a_out, b_out, c_out, d_out, sems):
    copies = [
        pltpu.make_async_copy(src, dst, sems.at[i])
        for i, (src, dst) in enumerate(((a, a_out), (b, b_out), (c, c_out), (d, d_out)))
    ]
    for copy in copies:
        copy.start()
    for copy in copies:
        copy.wait()


def relay_kernel(
    fwd_hbm, stash_hbm, cot_hbm, win_hbm, wout_hbm, gain_hbm,
    pass_fwd, pass_grad, gin_ref, gout_ref,
    gain_ref, xf, xs, xc, win, wout,
    nf, nb, slope, act_t, dpre_t, act, own_sum, parts, landed,
    mp_out, mp_in, own_terms, z_out,
    load_sem, swap_send, swap_recv, ag_send, ag_recv,
    mp_send, mp_recv, rs_send, rs_recv, z_send, z_recv,
):
    rows = pass_fwd.shape[0]
    tokens = 2 * rows
    hid, width = win.shape
    cols = gin_ref.shape[1]
    n_sec = lax.axis_size("section")
    sec, dp, mp = lax.axis_index("section"), lax.axis_index("dp"), lax.axis_index("mp")
    y, x = lax.div(dp, 2), lax.rem(dp, 2)
    flip_x, flip_y = y * 2 + (1 - x), (1 - y) * 2 + x
    across = (1 - y) * 2 + (1 - x)
    peer = {"mp": 1 - mp}
    after, before = {"section": lax.rem(sec + 1, n_sec)}, {"section": lax.rem(sec + n_sec - 1, n_sec)}
    partner = mp * flip_x + (1 - mp) * flip_y

    barrier = pltpu.get_barrier_semaphore()
    greeted = [after, before, peer] + [
        {"dp": chip, "mp": core} for chip in (flip_x, flip_y) for core in (mp, 1 - mp)
    ]
    for target in greeted:
        pl.semaphore_signal(barrier, inc=1, device_id=target, device_id_type=MESH)

    own, other = pl.ds(0, rows), pl.ds(rows, rows)
    near, far = pl.ds(0, tokens), pl.ds(tokens, tokens)
    local = (
        (gain_hbm, gain_ref), (fwd_hbm, xf.at[own]), (win_hbm, win), (wout_hbm, wout),
        (stash_hbm, xs.at[own]), (cot_hbm, xc.at[own]),
    )
    loads = [
        pltpu.make_async_copy(src, dst, load_sem.at[i]) for i, (src, dst) in enumerate(local)
    ]
    for load in loads:
        load.start()
    load_gain, load_fwd, load_win, load_wout, load_stash, load_cot = loads
    pl.semaphore_wait(barrier, len(greeted))

    swap_fwd = start_remote(fwd_hbm, xf.at[other], swap_send.at[0], swap_recv.at[0], peer)

    def column(block):
        return pl.ds(pl.multiple_of(block * cols, cols), cols)

    targets = (
        ({"dp": flip_x, "mp": 0}, (across, flip_x, dp, flip_y)),
        ({"dp": flip_y, "mp": 1}, (across, flip_y, dp, flip_x)),
    )
    slot = pl.ds(pl.multiple_of(tokens + mp * rows, rows), rows)
    gathers = []
    for d, (target, _) in enumerate(targets):
        gathers.append(
            start_remote(stash_hbm, xs.at[slot], ag_send.at[d, 0], ag_recv.at[mp, 0], target)
        )
    swap_stash = start_remote(stash_hbm, xs.at[other], swap_send.at[1], swap_recv.at[1], peer)
    swap_cot = start_remote(cot_hbm, xc.at[other], swap_send.at[2], swap_recv.at[2], peer)
    for i in range(4):
        for d, (target, order) in enumerate(targets):
            at = column(order[i])
            gathers.append(
                start_remote(
                    cot_hbm.at[:, at], xc.at[slot, at],
                    ag_send.at[d, 1 + i], ag_recv.at[mp, 1 + i], target,
                )
            )

    gathered = (partner, dp, (1 - mp) * flip_x + mp * flip_y, across)

    def await_gather(i):
        for core in range(2):
            rows_at = pl.ds(tokens + core * rows, rows)
            if i == 0:
                src, dst = stash_hbm, xs.at[rows_at]
            else:
                at = column(gathered[i - 1])
                src, dst = cot_hbm.at[:, at], xc.at[rows_at, at]
            remote(src, dst, ag_send.at[0, i], ag_recv.at[core, i], peer).wait_recv()

    step = tile_of(rows, 64)

    def normalise(source, target, first, count):
        def body(i, carry):
            at = pl.ds(pl.multiple_of(first + i * step, step), step)
            v = source[at, :].astype(jnp.float32)
            r = lax.rsqrt(jnp.mean(v * v, axis=-1, keepdims=True) + norm_eps)
            target[at, :] = (v * r * gain_ref[...]).astype(jnp.bfloat16)
            return carry

        lax.fori_loop(0, count // step, body, 0)

    block = tile_of(hid, 256)

    def backward_pre(span):
        def body(i, carry):
            at = pl.ds(pl.multiple_of(i * block, block), block)
            v = lax.dot_general(
                win[at, :], nb[span, :], NT, preferred_element_type=jnp.float32
            )
            square = v * v
            t = jnp.tanh(gelu_coef * (v + 0.044715 * square * v))
            act_t[at, span] = (0.5 * v * (1.0 + t)).astype(jnp.bfloat16)
            slope[at, :] = 0.5 * (1.0 + t) + 0.5 * v * (1.0 - t * t) * gelu_coef * (
                1.0 + 0.134145 * square
            )
            return carry

        lax.fori_loop(0, hid // block, body, 0)

    def backward_slope(span):
        def body(i, carry):
            at = pl.ds(pl.multiple_of(i * block, block), block)
            d_act = lax.dot_general(
                wout[at, :], xc[span, :], NT, preferred_element_type=jnp.float32
            )
            dpre_t[at, span] = (d_act * slope[at, :]).astype(jnp.bfloat16)
            return carry

        lax.fori_loop(0, hid // block, body, 0)

    def forward(span):
        def body(i, carry):
            at = pl.ds(pl.multiple_of(i * block, block), block)
            v = lax.dot_general(
                nf[span, :], win[at, :], NT, preferred_element_type=jnp.float32
            )
            t = jnp.tanh(gelu_coef * (v + 0.044715 * v * v * v))
            act[:, at] = (0.5 * v * (1.0 + t)).astype(jnp.bfloat16)
            return carry

        lax.fori_loop(0, hid // block, body, 0)
        return jnp.dot(
            act[...], wout[...], preferred_element_type=jnp.float32
        ).astype(jnp.bfloat16)

    load_gain.wait()
    load_fwd.wait()
    normalise(xf, nf, 0, rows)
    load_win.wait()
    load_wout.wait()
    swap_fwd.wait_recv()
    normalise(xf, nf, rows, rows)
    mp_out[1] = forward(other)
    swap_branch = start_remote(mp_out.at[1], mp_in.at[1], mp_send.at[1], mp_recv.at[1], peer)
    own_terms[1] = forward(own)
    swap_branch.wait_recv()

    def finish_forward(i, carry):
        at = pl.ds(pl.multiple_of(i * step, step), step)
        branch = own_terms[1, at, :].astype(jnp.float32) + mp_in[1, at, :].astype(jnp.float32)
        z_out[1, at, :] = (xf[at, :].astype(jnp.float32) + branch).astype(jnp.bfloat16)
        return carry

    lax.fori_loop(0, rows // step, finish_forward, 0)
    relay_fwd = start_remote(z_out.at[1], pass_fwd, z_send.at[1], z_recv.at[1], after)

    load_stash.wait()
    swap_stash.wait_recv()
    normalise(xs, nb, 0, tokens)
    backward_pre(near)
    load_cot.wait()
    swap_cot.wait_recv()
    backward_slope(near)

    def d_norm(span):
        return lax.dot_general(
            dpre_t[:, span], win[...], TN, preferred_element_type=jnp.float32
        ).astype(jnp.bfloat16)

    mp_out[0] = d_norm(other)
    swap_grad = start_remote(mp_out.at[0], mp_in.at[0], mp_send.at[0], mp_recv.at[0], peer)
    own_terms[0] = d_norm(own)
    swap_grad.wait_recv()

    def finish_grad(i, carry):
        at = pl.ds(pl.multiple_of(i * step, step), step)
        v = xs[at, :].astype(jnp.float32)
        r = lax.rsqrt(jnp.mean(v * v, axis=-1, keepdims=True) + norm_eps)
        push = (
            own_terms[0, at, :].astype(jnp.float32) + mp_in[0, at, :].astype(jnp.float32)
        ) * gain_ref[...]
        mixed = jnp.mean(v * push, axis=-1, keepdims=True)
        dx = xc[at, :].astype(jnp.float32) + r * push - v * (r * r * r * mixed)
        z_out[0, at, :] = dx.astype(jnp.bfloat16)
        return carry

    lax.fori_loop(0, rows // step, finish_grad, 0)
    relay_grad = start_remote(z_out.at[0], pass_grad, z_send.at[0], z_recv.at[0], before)

    operands = {OUT: (act_t, xc), IN: (dpre_t, nb)}
    size = hid // pieces
    bands = [pl.ds(p * size, size) for p in range(pieces)]
    sent = {}

    def product(g, p, owner):
        left, right = operands[g]
        return jnp.dot(
            left[bands[p], :], right[:, column(owner)], preferred_element_type=jnp.float32
        )

    def give(g):
        for p in range(pieces):
            parts[g, bands[p], :] = product(g, p, partner).astype(jnp.bfloat16)
            sent[g, p] = start_remote(
                parts.at[g, bands[p]], landed.at[g, bands[p]],
                rs_send.at[g, p], rs_recv.at[g, p], {"dp": partner},
            )

    def keep(g):
        for p in range(pieces):
            own_sum[g, bands[p], :] = product(g, p, dp)

    await_gather(0)
    normalise(xs, nb, tokens, tokens)
    backward_pre(far)
    await_gather(1)
    give(OUT)
    await_gather(2)
    keep(OUT)
    await_gather(3)
    await_gather(4)
    backward_slope(far)
    give(IN)
    keep(IN)

    for g, result in ((OUT, gout_ref), (IN, gin_ref)):
        for p in range(pieces):
            sent[g, p].wait_recv()
            result[bands[p], :] = (
                own_sum[g, bands[p], :] + landed[g, bands[p], :].astype(jnp.float32)
            ).astype(jnp.bfloat16)

    relay_grad.wait_recv()
    relay_fwd.wait_recv()
    for copy in [
        swap_fwd, swap_stash, swap_cot, *gathers, swap_grad, swap_branch,
        relay_grad, relay_fwd, *sent.values(),
    ]:
        copy.wait_send()


def relay_on_device(fwd_in, stash, cot, w_in, w_out, gain):
    rows, width = stash.shape[1:]
    hid = w_in.shape[1]
    tokens = rows * lax.axis_size("mp")
    cols = width // lax.axis_size("dp")
    bf16 = jnp.bfloat16
    vmem = pl.BlockSpec(memory_space=pltpu.VMEM)
    hbm = pl.BlockSpec(memory_space=pl.ANY)
    dma = pltpu.SemaphoreType.DMA
    held = (rows * width + hid * cols) * 2 * jnp.dtype(bf16).itemsize
    results = pl.pallas_call(
        relay_kernel,
        out_shape=(pltpu.VMEM((rows, width), bf16),) * 2 + (pltpu.VMEM((hid, cols), bf16),) * 2,
        in_specs=[hbm] * 6,
        out_specs=(vmem,) * 4,
        scratch_shapes=[
            pltpu.VMEM((1, width), jnp.float32),
            pltpu.VMEM((tokens, width), bf16),
            pltpu.VMEM((2 * tokens, width), bf16),
            pltpu.VMEM((2 * tokens, width), bf16),
            pltpu.VMEM((hid, width), bf16),
            pltpu.VMEM((hid, width), bf16),
            pltpu.VMEM((tokens, width), bf16),
            pltpu.VMEM((2 * tokens, width), bf16),
            pltpu.VMEM((hid, tokens), jnp.float32),
            pltpu.VMEM((hid, 2 * tokens), bf16),
            pltpu.VMEM((hid, 2 * tokens), bf16),
            pltpu.VMEM((rows, hid), bf16),
            pltpu.VMEM((2, hid, cols), jnp.float32),
            pltpu.VMEM((2, hid, cols), bf16),
            pltpu.VMEM((2, hid, cols), bf16),
            pltpu.VMEM((2, rows, width), bf16),
            pltpu.VMEM((2, rows, width), bf16),
            pltpu.VMEM((2, rows, width), bf16),
            pltpu.VMEM((2, rows, width), bf16),
            dma((6,)),
            dma((3,)),
            dma((3,)),
            dma((2, 5)),
            dma((2, 5)),
            dma((2,)),
            dma((2,)),
            dma((2, pieces)),
            dma((2, pieces)),
            dma((2,)),
            dma((2,)),
        ],
        compiler_params=pltpu.CompilerParams(
            collective_id=0, has_side_effects=True,
            vmem_limit_bytes=vmem_bytes - held - 2**17,
        ),
    )(fwd_in[0], stash[0], cot[0], w_in[0], w_out[0], gain)
    results = pl.pallas_call(
        write_kernel,
        out_shape=tuple(jax.ShapeDtypeStruct(r.shape, r.dtype) for r in results),
        in_specs=[vmem] * 4,
        out_specs=(hbm,) * 4,
        scratch_shapes=[dma((4,))],
        compiler_params=pltpu.CompilerParams(vmem_limit_bytes=4 * 2**20),
    )(*results)
    return tuple(r[None] for r in results)


def fits_relay(mesh):
    return mesh.shape["dp"] == 4 and mesh.shape["mp"] == 2 and mesh.shape["section"] > 1


def solution(mesh):
    in_specs = (
        P("section", ("dp", "mp"), None),
        P("section", ("dp", "mp"), None),
        P("section", ("dp", "mp"), None),
        P("section", "mp", None),
        P("section", "mp", None),
        P("section", None),
    )
    out_specs = (
        P("section", ("dp", "mp"), None),
        P("section", ("dp", "mp"), None),
        P("section", "mp", "dp"),
        P("section", "mp", "dp"),
    )
    return jax.shard_map(
        relay_on_device if fits_relay(mesh) else on_device,
        mesh=mesh,
        in_specs=in_specs,
        out_specs=out_specs,
        check_vma=False,
    )
```

time: 48.1 us -> 44.7 us (0.929)
  Pallas kernels: 47.3 us -> 43.9 us
    pallas_call x1 -> x0, Pallas kernels: 3.31 us -> none  [relay_on_device(): pl.pallas_call(swap_kernel, out_shape=(pltpu.VMEM((tokens, width), bf16),...]
where the time goes in v1:
time: 44.7 us; the launch traced here: 44.6 us
  Pallas kernels  43.9 us (98%)
  between operations  0.64 us (1%)
    pallas_call x1, Pallas kernels, relay_on_device(): pl.pallas_call(relay_kernel, out_shape=(pltpu.VMEM((rows, width), bf16),)...  42.6 us
    pallas_call x1, Pallas kernels, relay_on_device(): pl.pallas_call(write_kernel, out_shape=tuple((jax.ShapeDtypeStruct(r.shap...  1.35 us

profile of v1, /device:TPU:0, one launch (start us, length us, event | category | flops | bytes accessed | tf_op | source)
XLA Modules:
  0.0 44.6 jit_solution(964902186324580946)
XLA Ops:
  0.6 42.6 %shard_map.93 = (bf16[256,1024]{1,0:T(8,128)(2,1)S(1)}, bf16[256,1024]{1,0:T(8,128)(2,1)S(1)}, bf16[1024,256]{1,0:T(8,128)(2,1)S(1)}, bf16[1024,256]{1,0:T(8,128)(2,1)S(1)}) custom-call(bf16[256,1024]{1,0:T(8,128)(2,1)} %bitcast.11, bf16[256,1024]{1,0:T(8,128)(2,1)} %bitcast.12, bf16[256,1024]{1,0:T(8,128)(2,1)} %bitcast.13, bf16[1024,1024]{1,0:T(8,128)(2,1)} %bitcast.9, ...), custom_call_target="tpu_custom_call" | custom-call | tf_op jit(solution)/shard_map/pallas_call | solution.py:398
  43.2 1.3 %shard_map.94 = (bf16[256,1024]{1,0:T(8,128)(2,1)}, bf16[256,1024]{1,0:T(8,128)(2,1)}, bf16[1024,256]{1,0:T(8,128)(2,1)}, bf16[1024,256]{1,0:T(8,128)(2,1)}) custom-call(bf16[256,1024]{1,0:T(8,128)(2,1)S(1)} %get-tuple-element.12.a, bf16[256,1024]{1,0:T(8,128)(2,1)S(1)} %get-tuple-element.13.b, bf16[1024,256]{1,0:T(8,128)(2,1)S(1)} %get-tuple-element.14.c, ...), custom_call_target="tpu_custom_call" | custom-call | tf_op jit(solution)/shard_map/pallas_call | solution.py:440

commit v2 on v1

--- a/solution.py
+++ b/solution.py
@@ -148,7 +148,7 @@
     nf, nb, slope, act_t, dpre_t, act, own_sum, parts, landed,
     mp_out, mp_in, own_terms, z_out,
     load_sem, swap_send, swap_recv, ag_send, ag_recv,
-    mp_send, mp_recv, rs_send, rs_recv, z_send, z_recv,
+    mp_send, mp_recv, rs_send, rs_recv, z_send, z_recv, above, below, wrapped,
 ):
     rows = pass_fwd.shape[0]
     tokens = 2 * rows
@@ -164,27 +164,34 @@
     partner = mp * flip_x + (1 - mp) * flip_y
 
     barrier = pltpu.get_barrier_semaphore()
-    greeted = [after, before, peer] + [
+    greeted = [peer] + [
         {"dp": chip, "mp": core} for chip in (flip_x, flip_y) for core in (mp, 1 - mp)
     ]
+
+    def signal(sem, target):
+        pl.semaphore_signal(sem, inc=1, device_id=target, device_id_type=MESH)
+
     for target in greeted:
-        pl.semaphore_signal(barrier, inc=1, device_id=target, device_id_type=MESH)
+        signal(barrier, target)
+
+    @pl.when(sec < n_sec - 1)
+    def _():
+        signal(barrier, after)
 
     own, other = pl.ds(0, rows), pl.ds(rows, rows)
     near, far = pl.ds(0, tokens), pl.ds(tokens, tokens)
     local = (
-        (gain_hbm, gain_ref), (fwd_hbm, xf.at[own]), (win_hbm, win), (wout_hbm, wout),
-        (stash_hbm, xs.at[own]), (cot_hbm, xc.at[own]),
+        (stash_hbm, xs.at[own]), (cot_hbm, xc.at[own]), (fwd_hbm, xf.at[own]),
+        (gain_hbm, gain_ref), (win_hbm, win), (wout_hbm, wout),
     )
     loads = [
         pltpu.make_async_copy(src, dst, load_sem.at[i]) for i, (src, dst) in enumerate(local)
     ]
     for load in loads:
         load.start()
-    load_gain, load_fwd, load_win, load_wout, load_stash, load_cot = loads
-    pl.semaphore_wait(barrier, len(greeted))
-
-    swap_fwd = start_remote(fwd_hbm, xf.at[other], swap_send.at[0], swap_recv.at[0], peer)
+    load_stash, load_cot, load_fwd, load_gain, load_win, load_wout = loads
+    pl.semaphore_wait(barrier, len(greeted) + jnp.minimum(sec, 1))
+    load_stash.wait()
 
     def column(block):
         return pl.ds(pl.multiple_of(block * cols, cols), cols)
@@ -197,19 +204,31 @@
     gathers = []
     for d, (target, _) in enumerate(targets):
         gathers.append(
-            start_remote(stash_hbm, xs.at[slot], ag_send.at[d, 0], ag_recv.at[mp, 0], target)
+            start_remote(xs.at[own], xs.at[slot], ag_send.at[d, 0], ag_recv.at[mp, 0], target)
         )
-    swap_stash = start_remote(stash_hbm, xs.at[other], swap_send.at[1], swap_recv.at[1], peer)
-    swap_cot = start_remote(cot_hbm, xc.at[other], swap_send.at[2], swap_recv.at[2], peer)
+    load_fwd.wait()
+    swap_fwd = start_remote(xf.at[own], xf.at[other], swap_send.at[0], swap_recv.at[0], peer)
+    load_cot.wait()
+    swap_stash = start_remote(xs.at[own], xs.at[other], swap_send.at[1], swap_recv.at[1], peer)
+    swap_cot = start_remote(xc.at[own], xc.at[other], swap_send.at[2], swap_recv.at[2], peer)
     for i in range(4):
         for d, (target, order) in enumerate(targets):
             at = column(order[i])
             gathers.append(
                 start_remote(
-                    cot_hbm.at[:, at], xc.at[slot, at],
+                    xc.at[own, at], xc.at[slot, at],
                     ag_send.at[d, 1 + i], ag_recv.at[mp, 1 + i], target,
                 )
             )
+
+    @pl.when(sec > 0)
+    def _():
+        signal(above, before)
+
+    @pl.when((sec == 1) & (sec < n_sec - 1))
+    def _():
+        pl.semaphore_wait(above, 1)
+        signal(below, after)
 
     gathered = (partner, dp, (1 - mp) * flip_x + mp * flip_y, across)
 
@@ -217,10 +236,10 @@
         for core in range(2):
             rows_at = pl.ds(tokens + core * rows, rows)
             if i == 0:
-                src, dst = stash_hbm, xs.at[rows_at]
+                src, dst = xs.at[own], xs.at[rows_at]
             else:
                 at = column(gathered[i - 1])
-                src, dst = cot_hbm.at[:, at], xc.at[rows_at, at]
+                src, dst = xc.at[own, at], xc.at[rows_at, at]
             remote(src, dst, ag_send.at[0, i], ag_recv.at[core, i], peer).wait_recv()
 
     step = tile_of(rows, 64)
@@ -280,7 +299,6 @@
         ).astype(jnp.bfloat16)
 
     load_gain.wait()
-    load_fwd.wait()
     normalise(xf, nf, 0, rows)
     load_win.wait()
     load_wout.wait()
@@ -288,6 +306,13 @@
     normalise(xf, nf, rows, rows)
     mp_out[1] = forward(other)
     swap_branch = start_remote(mp_out.at[1], mp_in.at[1], mp_send.at[1], mp_recv.at[1], peer)
+
+    @pl.when((sec > 1) & (sec < n_sec - 1))
+    def _():
+        pl.semaphore_wait(above, 1)
+        pl.semaphore_wait(below, 1)
+        signal(below, after)
+
     own_terms[1] = forward(own)
     swap_branch.wait_recv()
 
@@ -298,13 +323,25 @@
         return carry
 
     lax.fori_loop(0, rows // step, finish_forward, 0)
+
+    @pl.when(sec == 0)
+    def _():
+        pl.semaphore_wait(above, 1)
+
+    if n_sec > 2:
+        @pl.when(sec == n_sec - 1)
+        def _():
+            pl.semaphore_wait(below, 1)
+
+    @pl.when(sec == n_sec - 1)
+    def _():
+        signal(wrapped, after)
+
     relay_fwd = start_remote(z_out.at[1], pass_fwd, z_send.at[1], z_recv.at[1], after)
 
-    load_stash.wait()
     swap_stash.wait_recv()
     normalise(xs, nb, 0, tokens)
     backward_pre(near)
-    load_cot.wait()
     swap_cot.wait_recv()
     backward_slope(near)
 
@@ -331,6 +368,11 @@
         return carry
 
     lax.fori_loop(0, rows // step, finish_grad, 0)
+
+    @pl.when(sec == 0)
+    def _():
+        pl.semaphore_wait(wrapped, 1)
+
     relay_grad = start_remote(z_out.at[0], pass_grad, z_send.at[0], z_recv.at[0], before)
 
     operands = {OUT: (act_t, xc), IN: (dpre_t, nb)}
@@ -431,6 +473,7 @@
             dma((2, pieces)),
             dma((2,)),
             dma((2,)),
+            *[pltpu.SemaphoreType.REGULAR] * 3,
         ],
         compiler_params=pltpu.CompilerParams(
             collective_id=0, has_side_effects=True,

time: 44.7 us -> 42 us (0.940)
  Pallas kernels: 43.9 us -> 41.2 us
    pallas_call x1, Pallas kernels: 42.6 us -> 39.9 us  [relay_on_device(): pl.pallas_call(relay_kernel, out_shape=(pltpu.VMEM((rows, width), bf16),)...]
where the time goes in v2:
time: 42 us; the launch traced here: 41.9 us
  Pallas kernels  41.2 us (98%)
  between operations  0.64 us (2%)
    pallas_call x1, Pallas kernels, relay_on_device(): pl.pallas_call(relay_kernel, out_shape=(pltpu.VMEM((rows, width), bf16),)...  39.9 us
    pallas_call x1, Pallas kernels, relay_on_device(): pl.pallas_call(write_kernel, out_shape=tuple((jax.ShapeDtypeStruct(r.shap...  1.35 us

profile of v2, /device:TPU:0, one launch (start us, length us, event | category | flops | bytes accessed | tf_op | source)
XLA Modules:
  0.0 41.9 jit_solution(8881368576996415253)
XLA Ops:
  0.6 39.9 %shard_map.93 = (bf16[256,1024]{1,0:T(8,128)(2,1)S(1)}, bf16[256,1024]{1,0:T(8,128)(2,1)S(1)}, bf16[1024,256]{1,0:T(8,128)(2,1)S(1)}, bf16[1024,256]{1,0:T(8,128)(2,1)S(1)}) custom-call(bf16[256,1024]{1,0:T(8,128)(2,1)} %bitcast.11, bf16[256,1024]{1,0:T(8,128)(2,1)} %bitcast.12, bf16[256,1024]{1,0:T(8,128)(2,1)} %bitcast.13, bf16[1024,1024]{1,0:T(8,128)(2,1)} %bitcast.9, ...), custom_call_target="tpu_custom_call" | custom-call | tf_op jit(solution)/shard_map/pallas_call | solution.py:440
  40.5 1.3 %shard_map.94 = (bf16[256,1024]{1,0:T(8,128)(2,1)}, bf16[256,1024]{1,0:T(8,128)(2,1)}, bf16[1024,256]{1,0:T(8,128)(2,1)}, bf16[1024,256]{1,0:T(8,128)(2,1)}) custom-call(bf16[256,1024]{1,0:T(8,128)(2,1)S(1)} %get-tuple-element.12.a, bf16[256,1024]{1,0:T(8,128)(2,1)S(1)} %get-tuple-element.13.b, bf16[1024,256]{1,0:T(8,128)(2,1)S(1)} %get-tuple-element.14.c, ...), custom_call_target="tpu_custom_call" | custom-call | tf_op jit(solution)/shard_map/pallas_call | solution.py:483

commit v3 on v2

--- a/solution.py
+++ b/solution.py
@@ -107,7 +107,7 @@
 NT = (((1,), (1,)), ((), ()))
 TN = (((0,), (0,)), ((), ()))
 OUT, IN = range(2)
-pieces = 2
+pieces = 4
 
 
 def tile_of(total, most):
@@ -148,7 +148,7 @@
     nf, nb, slope, act_t, dpre_t, act, own_sum, parts, landed,
     mp_out, mp_in, own_terms, z_out,
     load_sem, swap_send, swap_recv, ag_send, ag_recv,
-    mp_send, mp_recv, rs_send, rs_recv, z_send, z_recv, above, below, wrapped,
+    mp_send, mp_recv, rs_send, rs_recv, z_send, z_recv, above, below, wrapped, entered,
 ):
     rows = pass_fwd.shape[0]
     tokens = 2 * rows
@@ -164,15 +164,17 @@
     partner = mp * flip_x + (1 - mp) * flip_y
 
     barrier = pltpu.get_barrier_semaphore()
-    greeted = [peer] + [
-        {"dp": chip, "mp": core} for chip in (flip_x, flip_y) for core in (mp, 1 - mp)
-    ]
+    beside = [[{"dp": chip, "mp": core} for core in (mp, 1 - mp)] for chip in (flip_x, flip_y)]
 
     def signal(sem, target):
         pl.semaphore_signal(sem, inc=1, device_id=target, device_id_type=MESH)
 
-    for target in greeted:
-        signal(barrier, target)
+    signal(barrier, peer)
+    for low, targets in zip((x == 0, y == 0), beside):
+        @pl.when(low)
+        def _(targets=targets):
+            for target in targets:
+                signal(barrier, target)
 
     @pl.when(sec < n_sec - 1)
     def _():
@@ -190,7 +192,13 @@
     for load in loads:
         load.start()
     load_stash, load_cot, load_fwd, load_gain, load_win, load_wout = loads
-    pl.semaphore_wait(barrier, len(greeted) + jnp.minimum(sec, 1))
+    pl.semaphore_wait(barrier, 1 + 2 * x + 2 * y + jnp.minimum(sec, 1))
+    for i, (high, targets) in enumerate(zip((x == 1, y == 1), beside)):
+        @pl.when(high)
+        def _(i=i, targets=targets):
+            for target in targets:
+                signal(entered.at[i], target)
+
     load_stash.wait()
 
     def column(block):
@@ -204,8 +212,19 @@
     gathers = []
     for d, (target, _) in enumerate(targets):
         gathers.append(
-            start_remote(xs.at[own], xs.at[slot], ag_send.at[d, 0], ag_recv.at[mp, 0], target)
+            remote(xs.at[own], xs.at[slot], ag_send.at[d, 0], ag_recv.at[mp, 0], target)
         )
+    for d, copy in enumerate(gathers):
+        @pl.when((x, y)[d] == 1)
+        def _(copy=copy):
+            copy.start()
+
+    for d, copy in enumerate(gathers):
+        @pl.when((x, y)[d] == 0)
+        def _(d=d, copy=copy):
+            pl.semaphore_wait(entered.at[d], 2)
+            copy.start()
+
     load_fwd.wait()
     swap_fwd = start_remote(xf.at[own], xf.at[other], swap_send.at[0], swap_recv.at[0], peer)
     load_cot.wait()
@@ -272,16 +291,18 @@
 
         lax.fori_loop(0, hid // block, body, 0)
 
-    def backward_slope(span):
+    def backward_slope(span, first, count):
+        size = tile_of(count, 256)
+
         def body(i, carry):
-            at = pl.ds(pl.multiple_of(i * block, block), block)
+            at = pl.ds(pl.multiple_of(first + i * size, size), size)
             d_act = lax.dot_general(
                 wout[at, :], xc[span, :], NT, preferred_element_type=jnp.float32
             )
             dpre_t[at, span] = (d_act * slope[at, :]).astype(jnp.bfloat16)
             return carry
 
-        lax.fori_loop(0, hid // block, body, 0)
+        lax.fori_loop(0, count // size, body, 0)
 
     def forward(span):
         def body(i, carry):
@@ -343,7 +364,7 @@
     normalise(xs, nb, 0, tokens)
     backward_pre(near)
     swap_cot.wait_recv()
-    backward_slope(near)
+    backward_slope(near, 0, hid)
 
     def d_norm(span):
         return lax.dot_general(
@@ -388,6 +409,8 @@
 
     def give(g):
         for p in range(pieces):
+            if g == IN:
+                backward_slope(far, p * size, size)
             parts[g, bands[p], :] = product(g, p, partner).astype(jnp.bfloat16)
             sent[g, p] = start_remote(
                 parts.at[g, bands[p]], landed.at[g, bands[p]],
@@ -407,7 +430,6 @@
     keep(OUT)
     await_gather(3)
     await_gather(4)
-    backward_slope(far)
     give(IN)
     keep(IN)
 
@@ -474,6 +496,7 @@
             dma((2,)),
             dma((2,)),
             *[pltpu.SemaphoreType.REGULAR] * 3,
+            pltpu.SemaphoreType.REGULAR((2,)),
         ],
         compiler_params=pltpu.CompilerParams(
             collective_id=0, has_side_effects=True,

time: 42 us -> 41.2 us (0.981)
  Pallas kernels: 41.2 us -> 40.4 us
    pallas_call x1, Pallas kernels: 39.9 us -> 39.1 us  [relay_on_device(): pl.pallas_call(relay_kernel, out_shape=(pltpu.VMEM((rows, width), bf16),)...]
where the time goes in v3:
time: 41.2 us; the launch traced here: 41.1 us
  Pallas kernels  40.4 us (98%)
  between operations  0.64 us (2%)
    pallas_call x1, Pallas kernels, relay_on_device(): pl.pallas_call(relay_kernel, out_shape=(pltpu.VMEM((rows, width), bf16),)...  39.1 us
    pallas_call x1, Pallas kernels, relay_on_device(): pl.pallas_call(write_kernel, out_shape=tuple((jax.ShapeDtypeStruct(r.shap...  1.35 us

profile of v3, /device:TPU:0, one launch (start us, length us, event | category | flops | bytes accessed | tf_op | source)
XLA Modules:
  0.0 41.1 jit_solution(2754535908513469355)
XLA Ops:
  0.6 39.1 %shard_map.93 = (bf16[256,1024]{1,0:T(8,128)(2,1)S(1)}, bf16[256,1024]{1,0:T(8,128)(2,1)S(1)}, bf16[1024,256]{1,0:T(8,128)(2,1)S(1)}, bf16[1024,256]{1,0:T(8,128)(2,1)S(1)}) custom-call(bf16[256,1024]{1,0:T(8,128)(2,1)} %bitcast.11, bf16[256,1024]{1,0:T(8,128)(2,1)} %bitcast.12, bf16[256,1024]{1,0:T(8,128)(2,1)} %bitcast.13, bf16[1024,1024]{1,0:T(8,128)(2,1)} %bitcast.9, ...), custom_call_target="tpu_custom_call" | custom-call | tf_op jit(solution)/shard_map/pallas_call | solution.py:462
  39.7 1.3 %shard_map.94 = (bf16[256,1024]{1,0:T(8,128)(2,1)}, bf16[256,1024]{1,0:T(8,128)(2,1)}, bf16[1024,256]{1,0:T(8,128)(2,1)}, bf16[1024,256]{1,0:T(8,128)(2,1)}) custom-call(bf16[256,1024]{1,0:T(8,128)(2,1)S(1)} %get-tuple-element.12.a, bf16[256,1024]{1,0:T(8,128)(2,1)S(1)} %get-tuple-element.13.b, bf16[1024,256]{1,0:T(8,128)(2,1)S(1)} %get-tuple-element.14.c, ...), custom_call_target="tpu_custom_call" | custom-call | tf_op jit(solution)/shard_map/pallas_call | solution.py:506

commit v4 on v3

--- a/solution.py
+++ b/solution.py
@@ -8,23 +8,19 @@
 norm_eps = 1e-05
 gelu_coef = 0.7978845608
 
-
 def shifted(x, axis, by):
     length = lax.axis_size(axis)
     return lax.ppermute(x, axis, [(i, (i + by) % length) for i in range(length)])
 
-
 def gelu_value(v):
     inner = jnp.tanh(gelu_coef * (v + 0.044715 * v * v * v))
     return 0.5 * v * (1.0 + inner)
-
 
 def gelu_slope(v):
     inner = jnp.tanh(gelu_coef * (v + 0.044715 * v * v * v))
     return 0.5 * (1.0 + inner) + 0.5 * v * (1.0 - inner * inner) * gelu_coef * (
         1.0 + 0.134145 * v * v
     )
-
 
 def prepare(x, w_first, gain_row):
     xf = x.astype(jnp.float32)
@@ -35,7 +31,6 @@
     )
     act = gelu_value(pre).astype(jnp.bfloat16)
     return (scale, normed, pre, act)
-
 
 def on_device(fwd_in, stash, cot, w_in, w_out, gain):
     x_fwd = fwd_in[0]
@@ -101,7 +96,6 @@
         sum_out.astype(jnp.bfloat16)[None],
     )
 
-
 MESH = pl.DeviceIdType.MESH
 vmem_bytes = 67_043_328
 NT = (((1,), (1,)), ((), ()))
@@ -109,26 +103,22 @@
 OUT, IN = range(2)
 pieces = 4
 
-
 def tile_of(total, most):
     size = min(total, most)
     while total % size:
         size //= 2
     return size
 
-
 def remote(src, dst, send, recv, target):
     return pltpu.make_async_remote_copy(
         src_ref=src, dst_ref=dst, send_sem=send, recv_sem=recv,
         device_id=target, device_id_type=MESH,
     )
 
-
 def start_remote(src, dst, send, recv, target):
     copy = remote(src, dst, send, recv, target)
     copy.start()
     return copy
-
 
 def write_kernel(a, b, c, d, a_out, b_out, c_out, d_out, sems):
     copies = [
@@ -139,7 +129,6 @@
         copy.start()
     for copy in copies:
         copy.wait()
-
 
 def relay_kernel(
     fwd_hbm, stash_hbm, cot_hbm, win_hbm, wout_hbm, gain_hbm,
@@ -169,7 +158,10 @@
     def signal(sem, target):
         pl.semaphore_signal(sem, inc=1, device_id=target, device_id_type=MESH)
 
-    signal(barrier, peer)
+    @pl.when(mp == 1)
+    def _():
+        signal(barrier, peer)
+
     for low, targets in zip((x == 0, y == 0), beside):
         @pl.when(low)
         def _(targets=targets):
@@ -192,15 +184,22 @@
     for load in loads:
         load.start()
     load_stash, load_cot, load_fwd, load_gain, load_win, load_wout = loads
-    pl.semaphore_wait(barrier, 1 + 2 * x + 2 * y + jnp.minimum(sec, 1))
+    awaited = 1 - mp + 2 * x + 2 * y + jnp.minimum(sec, 1)
+
+    @pl.when(awaited > 0)
+    def _():
+        pl.semaphore_wait(barrier, awaited)
+
+    @pl.when(mp == 0)
+    def _():
+        signal(entered.at[2], peer)
+
     for i, (high, targets) in enumerate(zip((x == 1, y == 1), beside)):
         @pl.when(high)
         def _(i=i, targets=targets):
             for target in targets:
                 signal(entered.at[i], target)
 
-    load_stash.wait()
-
     def column(block):
         return pl.ds(pl.multiple_of(block * cols, cols), cols)
 
@@ -212,7 +211,7 @@
     gathers = []
     for d, (target, _) in enumerate(targets):
         gathers.append(
-            remote(xs.at[own], xs.at[slot], ag_send.at[d, 0], ag_recv.at[mp, 0], target)
+            remote(stash_hbm, xs.at[slot], ag_send.at[d, 0], ag_recv.at[mp, 0], target)
         )
     for d, copy in enumerate(gathers):
         @pl.when((x, y)[d] == 1)
@@ -225,8 +224,13 @@
             pl.semaphore_wait(entered.at[d], 2)
             copy.start()
 
+    @pl.when(mp == 1)
+    def _():
+        pl.semaphore_wait(entered.at[2], 1)
+
     load_fwd.wait()
     swap_fwd = start_remote(xf.at[own], xf.at[other], swap_send.at[0], swap_recv.at[0], peer)
+    load_stash.wait()
     load_cot.wait()
     swap_stash = start_remote(xs.at[own], xs.at[other], swap_send.at[1], swap_recv.at[1], peer)
     swap_cot = start_remote(xc.at[own], xc.at[other], swap_send.at[2], swap_recv.at[2], peer)
@@ -433,21 +437,17 @@
     give(IN)
     keep(IN)
 
+    for copy in [swap_fwd, swap_stash, swap_cot, *gathers, swap_grad, swap_branch]:
+        copy.wait_send()
     for g, result in ((OUT, gout_ref), (IN, gin_ref)):
         for p in range(pieces):
-            sent[g, p].wait_recv()
+            if (g, p) == (IN, pieces - 1):
+                for copy in (relay_grad, relay_fwd):
+                    copy.wait()
+            sent[g, p].wait()
             result[bands[p], :] = (
                 own_sum[g, bands[p], :] + landed[g, bands[p], :].astype(jnp.float32)
             ).astype(jnp.bfloat16)
-
-    relay_grad.wait_recv()
-    relay_fwd.wait_recv()
-    for copy in [
-        swap_fwd, swap_stash, swap_cot, *gathers, swap_grad, swap_branch,
-        relay_grad, relay_fwd, *sent.values(),
-    ]:
-        copy.wait_send()
-
 
 def relay_on_device(fwd_in, stash, cot, w_in, w_out, gain):
     rows, width = stash.shape[1:]
@@ -496,7 +496,7 @@
             dma((2,)),
             dma((2,)),
             *[pltpu.SemaphoreType.REGULAR] * 3,
-            pltpu.SemaphoreType.REGULAR((2,)),
+            pltpu.SemaphoreType.REGULAR((3,)),
         ],
         compiler_params=pltpu.CompilerParams(
             collective_id=0, has_side_effects=True,
@@ -513,10 +513,8 @@
     )(*results)
     return tuple(r[None] for r in results)
 
-
 def fits_relay(mesh):
     return mesh.shape["dp"] == 4 and mesh.shape["mp"] == 2 and mesh.shape["section"] > 1
-
 
 def solution(mesh):
     in_specs = (

time: 41.2 us -> 40.5 us (0.983)
  Pallas kernels: 40.4 us -> 39.7 us
    pallas_call x1, Pallas kernels: 39.1 us -> 38.4 us  [relay_on_device(): pl.pallas_call(relay_kernel, out_shape=(pltpu.VMEM((rows, width), bf16),)...]
where the time goes in v4:
time: 40.5 us; the launch traced here: 40.4 us
  Pallas kernels  39.7 us (98%)
  between operations  0.64 us (2%)
    pallas_call x1, Pallas kernels, relay_on_device(): pl.pallas_call(relay_kernel, out_shape=(pltpu.VMEM((rows, width), bf16),)...  38.4 us
    pallas_call x1, Pallas kernels, relay_on_device(): pl.pallas_call(write_kernel, out_shape=tuple((jax.ShapeDtypeStruct(r.shap...  1.35 us

profile of v4, /device:TPU:0, one launch (start us, length us, event | category | flops | bytes accessed | tf_op | source)
XLA Modules:
  0.0 40.4 jit_solution(9030960295100913268)
XLA Ops:
  0.6 38.4 %shard_map.93 = (bf16[256,1024]{1,0:T(8,128)(2,1)S(1)}, bf16[256,1024]{1,0:T(8,128)(2,1)S(1)}, bf16[1024,256]{1,0:T(8,128)(2,1)S(1)}, bf16[1024,256]{1,0:T(8,128)(2,1)S(1)}) custom-call(bf16[256,1024]{1,0:T(8,128)(2,1)} %bitcast.11, bf16[256,1024]{1,0:T(8,128)(2,1)} %bitcast.12, bf16[256,1024]{1,0:T(8,128)(2,1)} %bitcast.13, bf16[1024,1024]{1,0:T(8,128)(2,1)} %bitcast.9, ...), custom_call_target="tpu_custom_call" | custom-call | tf_op jit(solution)/shard_map/pallas_call | solution.py:462
  39.0 1.3 %shard_map.94 = (bf16[256,1024]{1,0:T(8,128)(2,1)}, bf16[256,1024]{1,0:T(8,128)(2,1)}, bf16[1024,256]{1,0:T(8,128)(2,1)}, bf16[1024,256]{1,0:T(8,128)(2,1)}) custom-call(bf16[256,1024]{1,0:T(8,128)(2,1)S(1)} %get-tuple-element.12.a, bf16[256,1024]{1,0:T(8,128)(2,1)S(1)} %get-tuple-element.13.b, bf16[1024,256]{1,0:T(8,128)(2,1)S(1)} %get-tuple-element.14.c, ...), custom_call_target="tpu_custom_call" | custom-call | tf_op jit(solution)/shard_map/pallas_call | solution.py:506

commit v5 on v4

--- a/solution.py
+++ b/solution.py
@@ -181,24 +181,12 @@
     loads = [
         pltpu.make_async_copy(src, dst, load_sem.at[i]) for i, (src, dst) in enumerate(local)
     ]
-    for load in loads:
-        load.start()
     load_stash, load_cot, load_fwd, load_gain, load_win, load_wout = loads
     awaited = 1 - mp + 2 * x + 2 * y + jnp.minimum(sec, 1)
 
     @pl.when(awaited > 0)
     def _():
         pl.semaphore_wait(barrier, awaited)
-
-    @pl.when(mp == 0)
-    def _():
-        signal(entered.at[2], peer)
-
-    for i, (high, targets) in enumerate(zip((x == 1, y == 1), beside)):
-        @pl.when(high)
-        def _(i=i, targets=targets):
-            for target in targets:
-                signal(entered.at[i], target)
 
     def column(block):
         return pl.ds(pl.multiple_of(block * cols, cols), cols)
@@ -218,11 +206,34 @@
         def _(copy=copy):
             copy.start()
 
+    @pl.when(mp == 0)
+    def _():
+        signal(entered.at[2], peer)
+
+    for i, (high, cores) in enumerate(zip((x == 1, y == 1), beside)):
+        @pl.when(high)
+        def _(i=i, cores=cores):
+            for target in cores:
+                signal(entered.at[i], target)
+
+    for load in loads:
+        load.start()
+
     for d, copy in enumerate(gathers):
         @pl.when((x, y)[d] == 0)
         def _(d=d, copy=copy):
             pl.semaphore_wait(entered.at[d], 2)
             copy.start()
+
+    for i in range(4):
+        for d, (target, order) in enumerate(targets):
+            at = column(order[i])
+            gathers.append(
+                start_remote(
+                    cot_hbm.at[:, at], xc.at[slot, at],
+                    ag_send.at[d, 1 + i], ag_recv.at[mp, 1 + i], target,
+                )
+            )
 
     @pl.when(mp == 1)
     def _():
@@ -234,16 +245,6 @@
     load_cot.wait()
     swap_stash = start_remote(xs.at[own], xs.at[other], swap_send.at[1], swap_recv.at[1], peer)
     swap_cot = start_remote(xc.at[own], xc.at[other], swap_send.at[2], swap_recv.at[2], peer)
-    for i in range(4):
-        for d, (target, order) in enumerate(targets):
-            at = column(order[i])
-            gathers.append(
-                start_remote(
-                    xc.at[own, at], xc.at[slot, at],
-                    ag_send.at[d, 1 + i], ag_recv.at[mp, 1 + i], target,
-                )
-            )
-
     @pl.when(sec > 0)
     def _():
         signal(above, before)

time: 40.5 us -> 40.5 us (level)
  no operation moved by 1% of the time
where the time goes in v5:
time: 40.5 us; the launch traced here: 40.4 us
  Pallas kernels  39.7 us (98%)
  between operations  0.64 us (2%)
    pallas_call x1, Pallas kernels, relay_on_device(): pl.pallas_call(relay_kernel, out_shape=(pltpu.VMEM((rows, width), bf16),)...  38.4 us
    pallas_call x1, Pallas kernels, relay_on_device(): pl.pallas_call(write_kernel, out_shape=tuple((jax.ShapeDtypeStruct(r.shap...  1.35 us

profile of v5, /device:TPU:0, one launch (start us, length us, event | category | flops | bytes accessed | tf_op | source)
XLA Modules:
  0.0 40.4 jit_solution(1904812792999624132)
XLA Ops:
  0.6 38.4 %shard_map.93 = (bf16[256,1024]{1,0:T(8,128)(2,1)S(1)}, bf16[256,1024]{1,0:T(8,128)(2,1)S(1)}, bf16[1024,256]{1,0:T(8,128)(2,1)S(1)}, bf16[1024,256]{1,0:T(8,128)(2,1)S(1)}) custom-call(bf16[256,1024]{1,0:T(8,128)(2,1)} %bitcast.11, bf16[256,1024]{1,0:T(8,128)(2,1)} %bitcast.12, bf16[256,1024]{1,0:T(8,128)(2,1)} %bitcast.13, bf16[1024,1024]{1,0:T(8,128)(2,1)} %bitcast.9, ...), custom_call_target="tpu_custom_call" | custom-call | tf_op jit(solution)/shard_map/pallas_call | solution.py:463
  39.0 1.3 %shard_map.94 = (bf16[256,1024]{1,0:T(8,128)(2,1)}, bf16[256,1024]{1,0:T(8,128)(2,1)}, bf16[1024,256]{1,0:T(8,128)(2,1)}, bf16[1024,256]{1,0:T(8,128)(2,1)}) custom-call(bf16[256,1024]{1,0:T(8,128)(2,1)S(1)} %get-tuple-element.12.a, bf16[256,1024]{1,0:T(8,128)(2,1)S(1)} %get-tuple-element.13.b, bf16[1024,256]{1,0:T(8,128)(2,1)S(1)} %get-tuple-element.14.c, ...), custom_call_target="tpu_custom_call" | custom-call | tf_op jit(solution)/shard_map/pallas_call | solution.py:507

commit v6 on v5

--- a/solution.py
+++ b/solution.py
@@ -150,7 +150,7 @@
     across = (1 - y) * 2 + (1 - x)
     peer = {"mp": 1 - mp}
     after, before = {"section": lax.rem(sec + 1, n_sec)}, {"section": lax.rem(sec + n_sec - 1, n_sec)}
-    partner = mp * flip_x + (1 - mp) * flip_y
+    partner = mp * flip_y + (1 - mp) * flip_x
 
     barrier = pltpu.get_barrier_semaphore()
     beside = [[{"dp": chip, "mp": core} for core in (mp, 1 - mp)] for chip in (flip_x, flip_y)]
@@ -192,8 +192,8 @@
         return pl.ds(pl.multiple_of(block * cols, cols), cols)
 
     targets = (
-        ({"dp": flip_x, "mp": 0}, (across, flip_x, dp, flip_y)),
-        ({"dp": flip_y, "mp": 1}, (across, flip_y, dp, flip_x)),
+        ({"dp": flip_x, "mp": 1}, (across, flip_x, dp, flip_y)),
+        ({"dp": flip_y, "mp": 0}, (across, flip_y, dp, flip_x)),
     )
     slot = pl.ds(pl.multiple_of(tokens + mp * rows, rows), rows)
     gathers = []
@@ -254,7 +254,7 @@
         pl.semaphore_wait(above, 1)
         signal(below, after)
 
-    gathered = (partner, dp, (1 - mp) * flip_x + mp * flip_y, across)
+    gathered = (partner, dp, (1 - mp) * flip_y + mp * flip_x, across)
 
     def await_gather(i):
         for core in range(2):

time: 40.5 us -> 40.5 us (level)
  no operation moved by 1% of the time
where the time goes in v6:
time: 40.5 us; the launch traced here: 40.4 us
  Pallas kernels  39.7 us (98%)
  between operations  0.64 us (2%)
    pallas_call x1, Pallas kernels, relay_on_device(): pl.pallas_call(relay_kernel, out_shape=(pltpu.VMEM((rows, width), bf16),)...  38.4 us
    pallas_call x1, Pallas kernels, relay_on_device(): pl.pallas_call(write_kernel, out_shape=tuple((jax.ShapeDtypeStruct(r.shap...  1.35 us

profile of v6, /device:TPU:0, one launch (start us, length us, event | category | flops | bytes accessed | tf_op | source)
XLA Modules:
  0.0 40.4 jit_solution(11863092888225239460)
XLA Ops:
  0.6 38.4 %shard_map.93 = (bf16[256,1024]{1,0:T(8,128)(2,1)S(1)}, bf16[256,1024]{1,0:T(8,128)(2,1)S(1)}, bf16[1024,256]{1,0:T(8,128)(2,1)S(1)}, bf16[1024,256]{1,0:T(8,128)(2,1)S(1)}) custom-call(bf16[256,1024]{1,0:T(8,128)(2,1)} %bitcast.11, bf16[256,1024]{1,0:T(8,128)(2,1)} %bitcast.12, bf16[256,1024]{1,0:T(8,128)(2,1)} %bitcast.13, bf16[1024,1024]{1,0:T(8,128)(2,1)} %bitcast.9, ...), custom_call_target="tpu_custom_call" | custom-call | tf_op jit(solution)/shard_map/pallas_call | solution.py:463
  39.0 1.3 %shard_map.94 = (bf16[256,1024]{1,0:T(8,128)(2,1)}, bf16[256,1024]{1,0:T(8,128)(2,1)}, bf16[1024,256]{1,0:T(8,128)(2,1)}, bf16[1024,256]{1,0:T(8,128)(2,1)}) custom-call(bf16[256,1024]{1,0:T(8,128)(2,1)S(1)} %get-tuple-element.12.a, bf16[256,1024]{1,0:T(8,128)(2,1)S(1)} %get-tuple-element.13.b, bf16[1024,256]{1,0:T(8,128)(2,1)S(1)} %get-tuple-element.14.c, ...), custom_call_target="tpu_custom_call" | custom-call | tf_op jit(solution)/shard_map/pallas_call | solution.py:507
